TPU v7x, 32 devices: a whole 2x2x4 slice. The times are simulated.
32 devices in a mesh: slab: 4 (over x, core), rep: 8 (over z, y).
Axes of the slice: x: 2, y: 2, z: 4, core: 2. Of those that a mesh axis runs over, the one named last changes fastest.
Arguments:
- image: float32 [144, 256, 256], P('slab', 'rep'), may hold values from 0.5 to 2
- sensitivity: float32 [144, 256, 256], P('slab', 'rep'), may hold values from 0.5 to 2
- system_blocks: bfloat16 [512, 128, 1024], P(('slab', 'rep')), may hold values from 0 to 0.00390625
- tile_slab: int32 [512, 1], P(('slab', 'rep')), may hold values from 0 to 3; in each aligned block of 16 rows (0 to 15, 16 to 31, ...) at most 6 rows name the same one
- tile_block: int32 [512], P(('slab', 'rep')), may hold values from 0 to 2303
- background: bfloat16 [512, 128], P(('slab', 'rep')), may hold values from 0.19921875 to 1
Outputs:
- updated: float32 [144, 256, 256], P('slab', 'rep')
Inputs may be any that keep to these rules, and one draw needn't show every extreme that they name: `tile_slab`: among the 16 tiles of one device at most 6 view the same slab, and in some devices some slab is viewed by exactly 6.
All inputs are finite; a program needn't handle non-finite values.
Results may differ from a plain program's by a relative error of at most 0.0003.
Values may be sent and summed in bfloat16 or wider, within the bound.
A program may use at most 64 MiB of HBM per device.

v0:
```python
import jax
import jax.numpy as jnp
from jax import lax
from jax.sharding import PartitionSpec as P

CAP = 6


def local(image, sensitivity, system_blocks, tile_slab, tile_block, background):
    slab_count = lax.axis_size("slab")
    tiles_here, tile_rows, width = system_blocks.shape
    destination = tile_slab[:, 0]
    replica_total = lax.axis_size("rep")
    detector_plane_count, local_rows, column_count = image.shape
    local_blocks = image.astype(jnp.bfloat16).reshape(-1, width)
    per_plane = local_rows * replica_total * column_count // width
    per_owner = local_rows * column_count // width
    within = tile_block % per_plane
    plane_of = tile_block // per_plane
    owner_rep = within // per_owner
    local_id = plane_of * per_owner + within % per_owner
    key = destination * replica_total + owner_rep
    key_hot = (
        key[:, None] == jnp.arange(slab_count * replica_total, dtype=jnp.int32)[None, :]
    ).astype(jnp.int32)
    position_order = jnp.sum((jnp.cumsum(key_hot, axis=0) - key_hot) * key_hot, axis=1)
    id_buffer = (
        jnp.zeros((slab_count, replica_total, CAP), jnp.int32)
        .at[destination, owner_rep, position_order]
        .set(local_id)
    )
    asked = lax.all_to_all(
        lax.all_to_all(id_buffer, "slab", split_axis=0, concat_axis=0, tiled=True),
        "rep",
        split_axis=1,
        concat_axis=1,
        tiled=True,
    )
    served_requests = local_blocks[asked]
    returned = lax.all_to_all(
        lax.all_to_all(served_requests, "slab", split_axis=0, concat_axis=0, tiled=True),
        "rep",
        split_axis=1,
        concat_axis=1,
        tiled=True,
    )
    emission_cell_entries = returned[destination, owner_rep, position_order]
    forward_projection = jnp.einsum(
        "tev,tv->te", system_blocks, emission_cell_entries, preferred_element_type=jnp.float32
    )
    inverse_permutation = (1.0 / (forward_projection + background.astype(jnp.float32))).astype(
        jnp.bfloat16
    )
    own_back = jnp.einsum(
        "tev,te->tv", system_blocks, inverse_permutation, preferred_element_type=jnp.float32
    )
    back_buffer = (
        jnp.zeros((slab_count, replica_total, CAP, width), jnp.float32)
        .at[destination, owner_rep, position_order]
        .set(own_back)
    )
    received_tiles = lax.all_to_all(
        lax.all_to_all(back_buffer, "slab", split_axis=0, concat_axis=0, tiled=True),
        "rep",
        split_axis=1,
        concat_axis=1,
        tiled=True,
    )
    owned = (
        jnp.zeros(local_blocks.shape, jnp.float32)
        .at[asked.reshape(-1)]
        .add(received_tiles.reshape(-1, width))
    )
    return image * owned.reshape(image.shape) / sensitivity


def solution(mesh):
    return jax.shard_map(
        local,
        mesh=mesh,
        in_specs=(
            P("slab", "rep", None),
            P("slab", "rep", None),
            P(("slab", "rep"), None, None),
            P(("slab", "rep"), None),
            P(("slab", "rep")),
            P(("slab", "rep"), None),
        ),
        out_specs=P("slab", "rep", None),
        check_vma=False,
    )
```

profile of v0, /device:TPU:0, one launch (start us, length us, event | category | flops | bytes accessed | tf_op | source)
XLA Modules:
  0.0 104.5 jit_solution(2315465785091688998)
XLA Ops:
  0.0 0.8 fusion.8
  0.8 0.7 bitcast_add_fusion
  1.7 0.7 fusion.12
  2.4 1.5 %scatter_fusion = s32[4,8,6]{1,0,2:T(4,128)S(1)} fusion(s32[4,8,6]{1,0,2:T(4,128)S(1)} %broadcast.74, s32[16]{0:T(128)S(1)} %get-tuple-element.8, s32[16]{0:T(128)S(1)} %get-tuple-element.5), kind=kCustom, calls=%fused_computation.2 | custom fusion | bytes 384 | tf_op jit(solution)/shard_map/scatter | solution.py:30
  3.9 7.9 %all_to_all.30 = s32[4,8,6]{1,2,0:T(8,128)S(1)} all-to-all(s32[4,8,6]{1,2,0:T(8,128)S(1)} %copy.23), channel_id=1, replica_groups=mesh['slab'=4,'rep'=8] {'slab'}, dimensions={0} | all-to-all | bytes 1536 | tf_op jit(solution)/shard_map/all_to_all | solution.py:33
  11.8 0.7 copy.24
  12.5 5.8 %all-to-all-start.1 = ((s32[4,8,6]{2,0,1:T(4,128)}), s32[4,8,6]{2,0,1:T(4,128)S(1)}, u32[]{:S(2)}, u32[]{:S(2)}) async-start(s32[4,8,6]{2,0,1:T(4,128)} %copy.24), calls=%async_computation.1 | async-start | bytes 32768 | tf_op jit(solution)/shard_map/all_to_all | solution.py:32
  18.5 0.4 reshape.57
  18.8 6.1 %all-to-all-done.1 = s32[4,8,6]{2,0,1:T(4,128)S(1)} async-done(((s32[4,8,6]{2,0,1:T(4,128)}), s32[4,8,6]{2,0,1:T(4,128)S(1)}, u32[]{:S(2)}, u32[]{:S(2)}) %all-to-all-start.1) | async-done | bytes 800 | tf_op jit(solution)/shard_map/all_to_all | solution.py:32
  25.3 1.0 gather_fusion
  26.7 9.8 %all_to_all.31 = bf16[4,8,6,1024]{3,1,2,0:T(8,128)(2,1)S(1)} all-to-all(bf16[4,8,6,1024]{3,1,2,0:T(8,128)(2,1)S(1)} %copy.30), channel_id=1, replica_groups=mesh['slab'=4,'rep'=8] {'slab'}, dimensions={0} | all-to-all | bytes 786432 | tf_op jit(solution)/shard_map/all_to_all | solution.py:41
  36.8 14.4 %all_to_all.32 = bf16[4,8,6,1024]{3,0,2,1:T(4,128)(2,1)S(1)} all-to-all(bf16[4,8,6,1024]{3,0,2,1:T(4,128)(2,1)S(1)} %copy.31), channel_id=1, replica_groups=mesh['slab'=4,'rep'=8] {'rep'}, dimensions={1} | all-to-all | bytes 786432 | tf_op jit(solution)/shard_map/all_to_all | solution.py:40
  51.4 0.7 gather_fusion.1
  52.1 3.5 %fusion.2 = f32[16,1,128]{2,1,0:T(1,128)S(1)} fusion(bf16[16,128,1024]{2,1,0:T(8,128)(2,1)} %param.8, bf16[16,1024,1]{1,0,2:T(8,128)(2,1)S(1)} %bitcast.32), kind=kOutput, calls=%fused_computation.9 | convolution fusion | flops 4194304 | bytes 4235264 | tf_op jit(solution)/shard_map/tev,tv->te/dot_general | solution.py:48
  55.7 0.7 fusion.4
  56.4 1.6 %scatter_fusion.1 = f32[4,8,6,1024]{3,1,2,0:T(8,128)S(1)} fusion(f32[4,8,6,1024]{3,1,2,0:T(8,128)S(1)} %broadcast_in_dim.10, s32[16]{0:T(128)S(1)} %get-tuple-element.8, f32[16,1024]{1,0:T(8,128)S(1)} %bitcast.33), kind=kCustom, calls=%fused_computation.3 | custom fusion | bytes 196800 | tf_op jit(solution)/shard_map/scatter | solution.py:60
  58.0 14.0 %all_to_all.33 = f32[4,8,6,1024]{3,1,2,0:T(8,128)S(1)} all-to-all(f32[4,8,6,1024]{3,1,2,0:T(8,128)S(1)} %scatter_fusion.1), channel_id=1, replica_groups=mesh['slab'=4,'rep'=8] {'slab'}, dimensions={0} | all-to-all | bytes 1572864 | tf_op jit(solution)/shard_map/all_to_all | solution.py:63
  72.1 1.4 %copy.33 = f32[4,8,6,1024]{3,0,2,1:T(4,128)} copy(f32[4,8,6,1024]{3,1,2,0:T(8,128)S(1)} %all_to_all.33) | data formatting | bytes 1572864 | tf_op jit(solution)/shard_map/all_to_all | solution.py:63
  73.5 3.5 %all-to-all-start.5 = ((f32[4,8,6,1024]{3,0,2,1:T(4,128)}), f32[4,8,6,1024]{3,0,2,1:T(4,128)S(1)}, u32[]{:S(2)}, u32[]{:S(2)}) async-start(f32[4,8,6,1024]{3,0,2,1:T(4,128)} %copy.33), calls=%async_computation.5 | async-start | bytes 1572864 | tf_op jit(solution)/shard_map/all_to_all | solution.py:62
  77.1 19.9 %all-to-all-done.5 = f32[4,8,6,1024]{3,0,2,1:T(4,128)S(1)} async-done(((f32[4,8,6,1024]{3,0,2,1:T(4,128)}), f32[4,8,6,1024]{3,0,2,1:T(4,128)S(1)}, u32[]{:S(2)}, u32[]{:S(2)}) %all-to-all-start.5) | async-done | bytes 786464 | tf_op jit(solution)/shard_map/all_to_all | solution.py:62
  97.1 0.5 copy.34
  97.6 1.0 reshape.90
  98.6 3.0 %scatter_custom_fusion.2 = f32[288,1024]{1,0:T(8,128)S(1)} fusion(s32[192]{0:T(256)S(1)} %bitcast.36, f32[192,1024]{1,0:T(8,128)} %reshape.90, f32[]{:T(128)} %constant.55.clone.1), kind=kCustom, calls=%fused_computation.6 | custom fusion | flops 196608 | bytes 1180160 | tf_op jit(solution)/shard_map/scatter-add | solution.py:72
  101.9 2.6 %multiply_divide_fusion = f32[36,32,256]{2,1,0:T(8,128)} fusion(f32[36,32,256]{2,1,0:T(8,128)} %param.7, f32[36,32,256]{2,1,0:T(8,128)S(1)} %copy-done.1, f32[36,32,256]{2,1,0:T(8,128)S(1)} %reshape.59), kind=kLoop, calls=%fused_computation.5 | loop fusion | flops 589824 | bytes 4718592 | tf_op jit(solution)/shard_map/div | solution.py:74
  (28 shorter events, 2.2 us)
Async XLA Ops:
  0.0 18.4 %copy-start.1 = (f32[36,32,256]{2,1,0:T(8,128)S(1)}, f32[36,32,256]{2,1,0:T(8,128)}, u32[]{:S(2)}) copy-start(f32[36,32,256]{2,1,0:T(8,128)} %param.6) | copy-start | bytes 3538948
  12.5 12.4 %all-to-all-start.1 = ((s32[4,8,6]{2,0,1:T(4,128)}), s32[4,8,6]{2,0,1:T(4,128)S(1)}, u32[]{:S(2)}, u32[]{:S(2)}) async-start(s32[4,8,6]{2,0,1:T(4,128)} %copy.24), calls=%async_computation.1 | async-start | bytes 32768 | tf_op jit(solution)/shard_map/all_to_all | solution.py:32
  52.1 3.5 %copy-start.2 = (bf16[16,128]{1,0:T(8,128)(2,1)S(1)}, bf16[16,128]{1,0:T(8,128)(2,1)}, u32[]{:S(2)}) copy-start(bf16[16,128]{1,0:T(8,128)(2,1)} %param.11) | copy-start | bytes 12292
  52.1 3.6 %copy-start = (bf16[16,128,1024]{2,1,0:T(8,128)(2,1)S(1)}, bf16[16,128,1024]{2,1,0:T(8,128)(2,1)}, u32[]{:S(2)}) copy-start(bf16[16,128,1024]{2,1,0:T(8,128)(2,1)} %param.8) | copy-start | bytes 12582916
  73.5 23.6 %all-to-all-start.5 = ((f32[4,8,6,1024]{3,0,2,1:T(4,128)}), f32[4,8,6,1024]{3,0,2,1:T(4,128)S(1)}, u32[]{:S(2)}, u32[]{:S(2)}) async-start(f32[4,8,6,1024]{3,0,2,1:T(4,128)} %copy.33), calls=%async_computation.5 | async-start | bytes 1572864 | tf_op jit(solution)/shard_map/all_to_all | solution.py:62
where the time goes:
time: 105 us
  blocking collectives  46.1 us (44%)
  waiting for transfers between devices  26.1 us (25%)
  local copies, waits for them, and re-layouts  10.5 us (10%)
  starting transfers between devices  9.38 us (9%)
  other arithmetic  8.13 us (8%)
  matrix products  4.17 us (4%)
    all_to_all x1, waiting for transfers between devices, local(): lax.all_to_all(lax.all_to_all(back_buffer, 'slab', split_axis=0, concat_a...  19.9 us
    all_to_all x1, blocking collectives, local(): lax.all_to_all(lax.all_to_all(served_requests, 'slab', split_axis=0, conc...  14.4 us
    all_to_all x1, blocking collectives, local(): lax.all_to_all(back_buffer, 'slab', split_axis=0, concat_axis=0, tiled=True)  14 us
    all_to_all x1, blocking collectives, local(): lax.all_to_all(served_requests, 'slab', split_axis=0, concat_axis=0, tile...  9.8 us
    all_to_all x1, blocking collectives, local(): lax.all_to_all(id_buffer, 'slab', split_axis=0, concat_axis=0, tiled=True)  7.9 us
    all_to_all x1, waiting for transfers between devices, local(): lax.all_to_all(lax.all_to_all(id_buffer, 'slab', split_axis=0, concat_axi...  6.12 us
    all_to_all x1, starting transfers between devices, local(): lax.all_to_all(lax.all_to_all(id_buffer, 'slab', split_axis=0, concat_axi...  5.83 us
    all_to_all x1, starting transfers between devices, local(): lax.all_to_all(lax.all_to_all(back_buffer, 'slab', split_axis=0, concat_a...  3.55 us
  transfers between devices with their start and end apart: 2, of which 2 were waited for; matrix products, arithmetic and copies ran while one was open for 1% of the time, Pallas kernels for 0%

commit v1 on v0

v1 whole, which is shorter than its diff:
```python
import functools

import jax
import jax.numpy as jnp
from jax import lax
from jax.experimental import pallas as pl
from jax.experimental.pallas import tpu as pltpu
from jax.sharding import PartitionSpec as P

CAP = 6
LANES = 128
MESH = pl.DeviceIdType.MESH


def exchange_kernel(
    sizes, meta_ref, image_hbm, sys_hbm, bg_ref, asked_ref, back_ref,
    image_v, blocks_v, sys_v, mine_v, slot_v, mine_s, slot_s, asked_s, send_f, recv_f, bp_v, send_b,
    local_sem, id_sem, fetch_sem, back_sem,
):
    n, reps, tiles, block_rows = sizes
    me = lax.axis_index("slab") * reps + lax.axis_index("rep")
    lane_tiles = image_v.shape[1] // LANES

    def device(d):
        return (d // reps, d % reps)

    load_sys = pltpu.make_async_copy(sys_hbm, sys_v, local_sem.at[0])
    load_image = pltpu.make_async_copy(image_hbm, image_v, local_sem.at[1])
    load_image.start()
    load_sys.start()

    barrier = pltpu.get_barrier_semaphore()

    def greet(i, c):
        pl.semaphore_signal(barrier, inc=1, device_id=device((me + i) % n), device_id_type=MESH)
        return c

    lax.fori_loop(1, n, greet, 0)

    key = meta_ref[0:1, :]
    value = meta_ref[1:2, :]
    hot = key == lax.broadcasted_iota(jnp.int32, (n, LANES), 0)
    earlier = lax.broadcasted_iota(jnp.int32, (LANES, LANES), 0) < lax.broadcasted_iota(
        jnp.int32, (LANES, LANES), 1
    )
    rank = jnp.dot(
        jnp.where(hot, 1.0, 0.0).astype(jnp.bfloat16),
        jnp.where(earlier, 1.0, 0.0).astype(jnp.bfloat16),
        preferred_element_type=jnp.float32,
    ).astype(jnp.int32)
    lane = lax.broadcasted_iota(jnp.int32, (n, LANES), 1)
    table = jnp.zeros((n, LANES), jnp.int32)
    for k in range(CAP):
        picked = jnp.sum(jnp.where(hot & (rank == k), value, 0), axis=1, keepdims=True)
        table = jnp.where(lane == k, picked, table)
    mine_v[...] = table
    own_rank = jnp.sum(jnp.where(hot, rank, 0), axis=0, keepdims=True)
    away = key - me
    slot = jnp.where(away < 0, away + n, away) * CAP + own_rank
    slot_v[...] = jnp.broadcast_to(jnp.clip(slot, 0, n * CAP - 1), slot_v.shape)
    to_slot = pltpu.make_async_copy(slot_v, slot_s, local_sem.at[2])
    to_slot.start()
    to_mine = pltpu.make_async_copy(mine_v, mine_s, local_sem.at[3])
    to_mine.start()
    asked_ref[pl.ds(0, 1), :] = mine_v[pl.ds(me, 1), :]

    pl.semaphore_wait(barrier, n - 1)

    def id_copy(i):
        d = (me + i) % n
        return pltpu.make_async_remote_copy(
            src_ref=mine_v.at[pl.ds(d, 1)], dst_ref=asked_ref.at[pl.ds(i, 1)],
            send_sem=id_sem.at[0], recv_sem=id_sem.at[1],
            device_id=device(d), device_id_type=MESH,
        )

    def send_ids(i, c):
        id_copy(i).start()
        return c

    lax.fori_loop(1, n, send_ids, 0)
    to_slot.wait()
    to_mine.wait()
    load_image.wait()
    per_group = 8 // block_rows

    def cut(g, c):
        rows = image_v[pl.ds(pl.multiple_of(g * 8, 8), 8), :].astype(jnp.bfloat16).astype(jnp.float32)
        for u in range(per_group):
            blocks_v[g * per_group + u] = jnp.concatenate(
                [
                    rows[u * block_rows:(u + 1) * block_rows, h * LANES:(h + 1) * LANES]
                    for h in range(lane_tiles)
                ],
                axis=0,
            ).astype(jnp.bfloat16)
        return c

    lax.fori_loop(0, image_v.shape[0] // 8, cut, 0, unroll=4)
    rest = asked_ref.at[pl.ds(1, n - 1)]
    pltpu.make_async_copy(rest, rest, id_sem.at[1]).wait()
    to_asked = pltpu.make_async_copy(asked_ref, asked_s, local_sem.at[2])
    to_asked.start()
    to_asked.wait()

    def served(i, k):
        return blocks_v[jnp.maximum(asked_s[i, k] - 1, 0) // tiles]

    for k in range(CAP):
        recv_f[k] = served(0, k)

    def serve(i, c):
        for k in range(CAP):
            send_f[i * CAP + k] = served(i, k)
        span = pl.ds(i * CAP, CAP)
        pltpu.make_async_remote_copy(
            src_ref=send_f.at[span], dst_ref=recv_f.at[span],
            send_sem=fetch_sem.at[0], recv_sem=fetch_sem.at[1],
            device_id=device((me + n - i) % n), device_id_type=MESH,
        ).start()
        return c

    lax.fori_loop(1, n, serve, 0)
    background = jnp.transpose(bg_ref[...].astype(jnp.float32))
    load_sys.wait()
    others = recv_f.at[pl.ds(CAP, (n - 1) * CAP)]
    pltpu.make_async_copy(others, others, fetch_sem.at[1]).wait()

    for t in range(tiles):
        cells = recv_f[slot_s[0, t]].astype(jnp.float32)
        total = None
        for p in range(block_rows * lane_tiles):
            q = (p % block_rows) * lane_tiles + p // block_rows
            term = sys_v[t, :, q * LANES:(q + 1) * LANES].astype(jnp.float32) * cells[p:p + 1, :]
            total = term if total is None else total + term
        forward = jnp.sum(total, axis=1, keepdims=True)
        inverse = (1.0 / (forward + background[:, t:t + 1])).astype(jnp.bfloat16).astype(jnp.float32)
        parts = []
        for p in range(block_rows * lane_tiles):
            q = (p % block_rows) * lane_tiles + p // block_rows
            term = sys_v[t, :, q * LANES:(q + 1) * LANES].astype(jnp.float32) * inverse
            parts.append(jnp.sum(term, axis=0, keepdims=True))
        bp_v[t] = jnp.concatenate(parts, axis=0)

    def routed(d, k):
        return bp_v[jnp.maximum(mine_s[d, k] - 1, 0) % tiles]

    for k in range(CAP):
        back_ref[k] = routed(me, k)

    def give(i, c):
        d = (me + i) % n
        for k in range(CAP):
            send_b[i * CAP + k] = routed(d, k)
        span = pl.ds(i * CAP, CAP)
        pltpu.make_async_remote_copy(
            src_ref=send_b.at[span], dst_ref=back_ref.at[span],
            send_sem=back_sem.at[0], recv_sem=back_sem.at[1],
            device_id=device(d), device_id_type=MESH,
        ).start()
        return c

    lax.fori_loop(1, n, give, 0)
    pltpu.make_async_copy(mine_v.at[pl.ds(1, n - 1)], mine_v.at[pl.ds(1, n - 1)], id_sem.at[0]).wait()
    sent = send_f.at[pl.ds(CAP, (n - 1) * CAP)]
    pltpu.make_async_copy(sent, sent, fetch_sem.at[0]).wait()
    given = send_b.at[pl.ds(CAP, (n - 1) * CAP)]
    pltpu.make_async_copy(given, given, back_sem.at[0]).wait()
    landed = back_ref.at[pl.ds(CAP, (n - 1) * CAP)]
    pltpu.make_async_copy(landed, landed, back_sem.at[1]).wait()


def update_kernel(sizes, asked_s, back_ref, image_ref, sens_ref, out_ref, sums_v):
    n, tiles, block_rows = sizes
    lane_tiles = out_ref.shape[1] // LANES
    per_group = 8 // block_rows
    sums_v[...] = jnp.zeros_like(sums_v)

    def add(i, k):
        if k == CAP:
            return
        value = asked_s[i, k]

        @pl.when(value > 0)
        def _():
            sums_v[(value - 1) // tiles] += back_ref[i * CAP + k]
            add(i, k + 1)

    def one(i, c):
        add(i, 0)
        return c

    lax.fori_loop(0, n, one, 0)

    def finish(g, c):
        rows = pl.ds(pl.multiple_of(g * 8, 8), 8)
        sums = [sums_v[g * per_group + u] for u in range(per_group)]
        for h in range(lane_tiles):
            cols = slice(h * LANES, (h + 1) * LANES)
            total = jnp.concatenate([s[h * block_rows:(h + 1) * block_rows] for s in sums], axis=0)
            out_ref[rows, cols] = image_ref[rows, cols] * total / sens_ref[rows, cols]
        return c

    lax.fori_loop(0, out_ref.shape[0] // 8, finish, 0, unroll=4)


def local(image, sensitivity, system_blocks, tile_slab, tile_block, background):
    slabs, reps = lax.axis_size("slab"), lax.axis_size("rep")
    n = slabs * reps
    tiles, events, width = system_blocks.shape
    planes, rows, cols = image.shape
    block_rows = width // cols
    per_owner = rows // block_rows
    per_plane = per_owner * reps
    within = tile_block % per_plane
    key = tile_slab[:, 0] * reps + within // per_owner
    local_id = (tile_block // per_plane) * per_owner + within % per_owner
    value = local_id * tiles + jnp.arange(tiles, dtype=jnp.int32) + 1
    meta = jnp.full((8, LANES), -1, jnp.int32).at[0, :tiles].set(key).at[1, :tiles].set(value)
    image2 = image.reshape(planes * rows, cols)
    sens2 = sensitivity.reshape(planes * rows, cols)
    sub = width // LANES

    vmem = pl.BlockSpec(memory_space=pltpu.VMEM)
    hbm = pl.BlockSpec(memory_space=pl.ANY)
    asked, back = pl.pallas_call(
        functools.partial(exchange_kernel, (n, reps, tiles, block_rows)),
        out_shape=(
            jax.ShapeDtypeStruct((n, LANES), jnp.int32),
            jax.ShapeDtypeStruct((n * CAP, sub, LANES), jnp.float32),
        ),
        in_specs=[vmem, hbm, hbm, vmem],
        out_specs=(vmem, vmem),
        scratch_shapes=[
            pltpu.VMEM(image2.shape, jnp.float32),
            pltpu.VMEM((planes * per_owner, sub, LANES), jnp.bfloat16),
            pltpu.VMEM(system_blocks.shape, jnp.bfloat16),
            pltpu.VMEM((n, LANES), jnp.int32),
            pltpu.VMEM((8, LANES), jnp.int32),
            pltpu.SMEM((n, LANES), jnp.int32),
            pltpu.SMEM((8, LANES), jnp.int32),
            pltpu.SMEM((n, LANES), jnp.int32),
            pltpu.VMEM((n * CAP, sub, LANES), jnp.bfloat16),
            pltpu.VMEM((n * CAP, sub, LANES), jnp.bfloat16),
            pltpu.VMEM((tiles, sub, LANES), jnp.float32),
            pltpu.VMEM((n * CAP, sub, LANES), jnp.float32),
            pltpu.SemaphoreType.DMA((4,)),
            pltpu.SemaphoreType.DMA((2,)),
            pltpu.SemaphoreType.DMA((2,)),
            pltpu.SemaphoreType.DMA((2,)),
        ],
        compiler_params=pltpu.CompilerParams(
            collective_id=0, has_side_effects=True, vmem_limit_bytes=48 * 1024 * 1024
        ),
    )(meta, image2, system_blocks, background)
    updated = pl.pallas_call(
        functools.partial(update_kernel, (n, tiles, block_rows)),
        out_shape=jax.ShapeDtypeStruct(image2.shape, jnp.float32),
        in_specs=[pl.BlockSpec(memory_space=pltpu.SMEM), vmem, vmem, vmem],
        out_specs=vmem,
        scratch_shapes=[pltpu.VMEM((planes * per_owner, sub, LANES), jnp.float32)],
        compiler_params=pltpu.CompilerParams(vmem_limit_bytes=48 * 1024 * 1024),
    )(asked, back, image2, sens2)
    return updated.reshape(image.shape)


def solution(mesh):
    return jax.shard_map(
        local,
        mesh=mesh,
        in_specs=(
            P("slab", "rep", None),
            P("slab", "rep", None),
            P(("slab", "rep"), None, None),
            P(("slab", "rep"), None),
            P(("slab", "rep")),
            P(("slab", "rep"), None),
        ),
        out_specs=P("slab", "rep", None),
        check_vma=False,
    )
```

time: 105 us -> 51.7 us (0.49)
  blocking collectives: 46.1 us -> 0 us
  Pallas kernels: 0 us -> 45.7 us
  waiting for transfers between devices: 26.1 us -> 0 us
  starting transfers between devices: 9.38 us -> 0 us
  other arithmetic: 8.13 us -> 1.34 us
  local copies, waits for them, and re-layouts: 10.5 us -> 4.34 us
  matrix products: 4.17 us -> 0 us
    all_to_all x4 -> x0, blocking collectives: 46.1 us -> none  [the longest x1 14.4 us: local(): lax.all_to_all(lax.all_to_all(served_requests, 'slab', split_axis=0, conc...]
    pallas_call x0 -> x2, Pallas kernels: none -> 45.7 us  [the longest x1 42.7 us: local(): pl.pallas_call(functools.partial(exchange_kernel, (n, reps, tiles, block_...]
    all_to_all x2 -> x0, waiting for transfers between devices: 26.1 us -> none  [the longest x1 19.9 us: local(): lax.all_to_all(lax.all_to_all(back_buffer, 'slab', split_axis=0, concat_a...]
    all_to_all x2 -> x0, starting transfers between devices: 9.38 us -> none  [the longest x1 5.83 us: local(): lax.all_to_all(lax.all_to_all(id_buffer, 'slab', split_axis=0, concat_axi...]
    dot_general x2 -> x0, matrix products: 4.17 us -> none  [the longest x1 3.52 us: local(): jnp.einsum('tev,tv->te', system_blocks, emission_cell_entries, preferred_...]
    unnamed x6 -> x10, local copies, waits for them, and re-layouts: 0.02 us -> 4.15 us
    all_to_all x7 -> x0, local copies, waits for them, and re-layouts: 3.2 us -> none  [the longest x1 1.39 us: local(): lax.all_to_all(back_buffer, 'slab', split_axis=0, concat_axis=0, tiled=True)]
    scatter-add x1 -> x0, other arithmetic: 3 us -> none  [local(): owned = jnp.zeros(local_blocks.shape, jnp.float32).at[asked.reshape(-1)]....]
  transfers between devices with their start and end apart: 2 -> 0, of which waited for: 2 -> 0; matrix products, arithmetic and copies ran while one was open for 1% -> 0% of each run, Pallas kernels for 0% -> 0%
where the time goes in v1:
time: 51.7 us; the launch traced here: 51.5 us
  Pallas kernels  45.7 us (88%)
  local copies, waits for them, and re-layouts  4.34 us (8%)
  other arithmetic  1.34 us (3%)
    pallas_call x1, Pallas kernels, local(): pl.pallas_call(functools.partial(exchange_kernel, (n, reps, tiles, block_...  42.7 us
    unnamed x10, local copies, waits for them, and re-layouts  4.15 us
    pallas_call x1, Pallas kernels, local(): pl.pallas_call(functools.partial(update_kernel, (n, tiles, block_rows)),...  3 us
    another operation x2, other arithmetic  1.34 us

profile of v1, /device:TPU:0, one launch (start us, length us, event | category | flops | bytes accessed | tf_op | source)
XLA Modules:
  0.0 51.5 jit_solution(12176936492313852206)
XLA Ops:
  0.0 0.7 %add_bitcast_fusion = (s32[1,16]{1,0:T(1,128)S(1)}, s32[16]{0:T(128)S(1)}, s32[16]{0:T(128)S(1)}) fusion(s32[16]{0:T(128)} %param.14), kind=kLoop, calls=%fused_computation.13 | loop fusion | flops 560 | bytes 256 | tf_op jit(solution)/shard_map/reshape.40
  0.7 0.7 %fusion.1 = s32[1,16]{1,0:T(1,128)S(1)} fusion(s32[16,1]{0,1:T(1,128)} %param.13, s32[16]{0:T(128)S(1)} %get-tuple-element.34, s32[16]{0:T(128)S(1)} %get-tuple-element.35), kind=kLoop, calls=%fused_computation.12 | loop fusion | flops 304 | bytes 256 | tf_op jit(solution)/shard_map/reshape.57
  1.4 0.2 scatter.9.meta_ref
  1.6 0.0 copy-start
  1.6 1.3 %copy-done = f32[36,32,256]{2,1,0:T(8,128)S(1)} copy-done((f32[36,32,256]{2,1,0:T(8,128)S(1)}, f32[36,32,256]{2,1,0:T(8,128)}, u32[]{:S(2)}) %copy-start) | copy-done | bytes 1179672
  2.8 0.0 copy-start.2
  2.8 2.2 %copy-done.2 = bf16[16,128,1024]{2,1,0:T(8,128)(2,1)S(1)} copy-done((bf16[16,128,1024]{2,1,0:T(8,128)(2,1)S(1)}, bf16[16,128,1024]{2,1,0:T(8,128)(2,1)}, u32[]{:S(2)}) %copy-start.2) | copy-done | bytes 4194328
  5.0 0.0 copy-start.4
  5.0 0.7 %copy-done.4 = bf16[16,128]{1,0:T(8,128)(2,1)S(1)} copy-done((bf16[16,128]{1,0:T(8,128)(2,1)S(1)}, bf16[16,128]{1,0:T(8,128)(2,1)}, u32[]{:S(2)}) %copy-start.4) | copy-done | bytes 4120
  5.7 0.0 copy-start.1
  5.7 0.0 copy-start.3
  5.7 42.7 %shard_map.64 = (s32[32,128]{1,0:T(8,128)S(1)}, f32[192,8,128]{2,1,0:T(8,128)S(1)}) custom-call(s32[8,128]{1,0:T(8,128)S(1)} %scatter.9.meta_ref, f32[1152,256]{1,0:T(8,128)S(1)} %bitcast.11, bf16[16,128,1024]{2,1,0:T(8,128)(2,1)S(1)} %copy-done.2, bf16[16,128]{1,0:T(8,128)(2,1)S(1)} %copy-done.4), custom_call_target="tpu_custom_call" | custom-call | tf_op jit(solution)/shard_map/pallas_call | solution.py:226
  48.4 0.0 copy-done.1
  48.5 0.0 copy-done.3
  48.5 3.0 %shard_map.65 = f32[1152,256]{1,0:T(8,128)} custom-call(s32[32,128]{1,0:T(8,128)S(1)} %get-tuple-element.31.asked_s, f32[192,8,128]{2,1,0:T(8,128)S(1)} %get-tuple-element.32.back_ref, f32[1152,256]{1,0:T(8,128)S(1)} %bitcast.12, f32[1152,256]{1,0:T(8,128)S(1)} %bitcast.13), custom_call_target="tpu_custom_call" | custom-call | tf_op jit(solution)/shard_map/pallas_call | solution.py:256
  (1 shorter events, 0.0 us)
Async XLA Ops:
  1.6 1.3 %copy-start = (f32[36,32,256]{2,1,0:T(8,128)S(1)}, f32[36,32,256]{2,1,0:T(8,128)}, u32[]{:S(2)}) copy-start(f32[36,32,256]{2,1,0:T(8,128)} %param.10) | copy-start | bytes 3538948
  2.8 2.2 %copy-start.2 = (bf16[16,128,1024]{2,1,0:T(8,128)(2,1)S(1)}, bf16[16,128,1024]{2,1,0:T(8,128)(2,1)}, u32[]{:S(2)}) copy-start(bf16[16,128,1024]{2,1,0:T(8,128)(2,1)} %sys_hbm.1) | copy-start | bytes 12582916
  5.0 0.7 %copy-start.4 = (bf16[16,128]{1,0:T(8,128)(2,1)S(1)}, bf16[16,128]{1,0:T(8,128)(2,1)}, u32[]{:S(2)}) copy-start(bf16[16,128]{1,0:T(8,128)(2,1)} %bg_ref.1) | copy-start | bytes 12292
  5.7 42.7 %copy-start.1 = (f32[36,32,256]{2,1,0:T(8,128)S(1)}, f32[36,32,256]{2,1,0:T(8,128)}, u32[]{:S(2)}) copy-start(f32[36,32,256]{2,1,0:T(8,128)} %param.10) | copy-start | bytes 3538948
  5.7 42.8 %copy-start.3 = (f32[36,32,256]{2,1,0:T(8,128)S(1)}, f32[36,32,256]{2,1,0:T(8,128)}, u32[]{:S(2)}) copy-start(f32[36,32,256]{2,1,0:T(8,128)} %param.11) | copy-start | bytes 3538948

commit v2 on v1

--- a/solution.py
+++ b/solution.py
@@ -8,16 +8,24 @@
 from jax.sharding import PartitionSpec as P
 
 CAP = 6
+LEVELS = 65535.0
+HALF = 32768
 LANES = 128
 MESH = pl.DeviceIdType.MESH
 
 
+def split(x, size):
+    if size & (size - 1):
+        return x // size, x % size
+    return x >> (size.bit_length() - 1), x & (size - 1)
+
+
 def exchange_kernel(
-    sizes, meta_ref, image_hbm, sys_hbm, bg_ref, asked_ref, back_ref,
-    image_v, blocks_v, sys_v, mine_v, slot_v, mine_s, slot_s, asked_s, send_f, recv_f, bp_v, send_b,
-    local_sem, id_sem, fetch_sem, back_sem,
+    sizes, slab_hbm, block_hbm, image_hbm, sys_hbm, bg_hbm, asked_ref, scale_ref, back_ref,
+    slab_v, block_v, bg_v, scale_v, image_v, blocks_v, sys_v, mine_v, slot_v, mine_s, slot_s, asked_s, send_f, recv_f, bp_v, send_b,
+    local_sem, id_sem, fetch_sem, back_sem, scale_sem,
 ):
-    n, reps, tiles, block_rows = sizes
+    n, reps, tiles, block_rows, per_owner = sizes
     me = lax.axis_index("slab") * reps + lax.axis_index("rep")
     lane_tiles = image_v.shape[1] // LANES
 
@@ -26,8 +34,11 @@
 
     load_sys = pltpu.make_async_copy(sys_hbm, sys_v, local_sem.at[0])
     load_image = pltpu.make_async_copy(image_hbm, image_v, local_sem.at[1])
-    load_image.start()
-    load_sys.start()
+    load_slab = pltpu.make_async_copy(slab_hbm, slab_v, local_sem.at[4])
+    load_block = pltpu.make_async_copy(block_hbm, block_v, local_sem.at[5])
+    load_bg = pltpu.make_async_copy(bg_hbm, bg_v, local_sem.at[6])
+    for load in (load_slab, load_block, load_image, load_bg, load_sys):
+        load.start()
 
     barrier = pltpu.get_barrier_semaphore()
 
@@ -37,27 +48,35 @@
 
     lax.fori_loop(1, n, greet, 0)
 
-    key = meta_ref[0:1, :]
-    value = meta_ref[1:2, :]
-    hot = key == lax.broadcasted_iota(jnp.int32, (n, LANES), 0)
-    earlier = lax.broadcasted_iota(jnp.int32, (LANES, LANES), 0) < lax.broadcasted_iota(
-        jnp.int32, (LANES, LANES), 1
-    )
+    load_slab.wait()
+    load_block.wait()
+    block = block_v[...]
+    plane, within = split(block, per_owner * reps)
+    owner, offset = split(within, per_owner)
+    key = slab_v[...] * reps + owner
+    value = (plane * per_owner + offset) * tiles + lax.broadcasted_iota(jnp.int32, (1, tiles), 1) + 1
+    hot = key == lax.broadcasted_iota(jnp.int32, (n, tiles), 0)
+    square = (tiles, tiles)
+    earlier = lax.broadcasted_iota(jnp.int32, square, 0) < lax.broadcasted_iota(jnp.int32, square, 1)
     rank = jnp.dot(
         jnp.where(hot, 1.0, 0.0).astype(jnp.bfloat16),
         jnp.where(earlier, 1.0, 0.0).astype(jnp.bfloat16),
         preferred_element_type=jnp.float32,
     ).astype(jnp.int32)
     lane = lax.broadcasted_iota(jnp.int32, (n, LANES), 1)
-    table = jnp.zeros((n, LANES), jnp.int32)
-    for k in range(CAP):
-        picked = jnp.sum(jnp.where(hot & (rank == k), value, 0), axis=1, keepdims=True)
-        table = jnp.where(lane == k, picked, table)
-    mine_v[...] = table
+
+    def tabled(row, zero):
+        table = jnp.full((n, LANES), zero)
+        for k in range(CAP):
+            picked = jnp.sum(jnp.where(hot & (rank == k), row, zero), axis=1, keepdims=True)
+            table = jnp.where(lane == k, picked, table)
+        return table
+
+    mine_v[...] = tabled(value, jnp.int32(0))
     own_rank = jnp.sum(jnp.where(hot, rank, 0), axis=0, keepdims=True)
     away = key - me
     slot = jnp.where(away < 0, away + n, away) * CAP + own_rank
-    slot_v[...] = jnp.broadcast_to(jnp.clip(slot, 0, n * CAP - 1), slot_v.shape)
+    slot_v[0:1, 0:tiles] = jnp.clip(slot, 0, n * CAP - 1)
     to_slot = pltpu.make_async_copy(slot_v, slot_s, local_sem.at[2])
     to_slot.start()
     to_mine = pltpu.make_async_copy(mine_v, mine_s, local_sem.at[3])
@@ -121,11 +140,14 @@
         return c
 
     lax.fori_loop(1, n, serve, 0)
-    background = jnp.transpose(bg_ref[...].astype(jnp.float32))
+    load_bg.wait()
+    background = jnp.transpose(bg_v[...].astype(jnp.float32))
     load_sys.wait()
     others = recv_f.at[pl.ds(CAP, (n - 1) * CAP)]
     pltpu.make_async_copy(others, others, fetch_sem.at[1]).wait()
 
+    peaks = jnp.zeros((1, tiles), jnp.float32)
+    tile_lane = lax.broadcasted_iota(jnp.int32, (1, tiles), 1)
     for t in range(tiles):
         cells = recv_f[slot_s[0, t]].astype(jnp.float32)
         total = None
@@ -140,7 +162,12 @@
             q = (p % block_rows) * lane_tiles + p // block_rows
             term = sys_v[t, :, q * LANES:(q + 1) * LANES].astype(jnp.float32) * inverse
             parts.append(jnp.sum(term, axis=0, keepdims=True))
-        bp_v[t] = jnp.concatenate(parts, axis=0)
+        tile = jnp.concatenate(parts, axis=0)
+        peak = jnp.maximum(jnp.max(jnp.max(tile, axis=0, keepdims=True), axis=1, keepdims=True), 1e-33)
+        level = jnp.round(tile * (LEVELS / peak)).astype(jnp.int32) - HALF
+        bp_v[t] = jnp.clip(level, -HALF, HALF - 1).astype(jnp.int16)
+        peaks = jnp.where(tile_lane == t, peak, peaks)
+    scale_v[...] = tabled(peaks * (1.0 / LEVELS), jnp.float32(0))
 
     def routed(d, k):
         return bp_v[jnp.maximum(mine_s[d, k] - 1, 0) % tiles]
@@ -158,9 +185,18 @@
             send_sem=back_sem.at[0], recv_sem=back_sem.at[1],
             device_id=device(d), device_id_type=MESH,
         ).start()
-        return c
-
+        pltpu.make_async_remote_copy(
+            src_ref=scale_v.at[pl.ds(d, 1)], dst_ref=scale_ref.at[pl.ds(i, 1)],
+            send_sem=scale_sem.at[0], recv_sem=scale_sem.at[1],
+            device_id=device(d), device_id_type=MESH,
+        ).start()
+        return c
+
+    scale_ref[pl.ds(0, 1), :] = scale_v[pl.ds(me, 1), :]
     lax.fori_loop(1, n, give, 0)
+    scaled = scale_ref.at[pl.ds(1, n - 1)]
+    pltpu.make_async_copy(scaled, scaled, scale_sem.at[0]).wait()
+    pltpu.make_async_copy(scaled, scaled, scale_sem.at[1]).wait()
     pltpu.make_async_copy(mine_v.at[pl.ds(1, n - 1)], mine_v.at[pl.ds(1, n - 1)], id_sem.at[0]).wait()
     sent = send_f.at[pl.ds(CAP, (n - 1) * CAP)]
     pltpu.make_async_copy(sent, sent, fetch_sem.at[0]).wait()
@@ -170,7 +206,7 @@
     pltpu.make_async_copy(landed, landed, back_sem.at[1]).wait()
 
 
-def update_kernel(sizes, asked_s, back_ref, image_ref, sens_ref, out_ref, sums_v):
+def update_kernel(sizes, asked_s, scale_s, back_ref, image_ref, sens_ref, out_ref, sums_v):
     n, tiles, block_rows = sizes
     lane_tiles = out_ref.shape[1] // LANES
     per_group = 8 // block_rows
@@ -183,7 +219,8 @@
 
         @pl.when(value > 0)
         def _():
-            sums_v[(value - 1) // tiles] += back_ref[i * CAP + k]
+            level = back_ref[i * CAP + k].astype(jnp.int32) + HALF
+            sums_v[(value - 1) // tiles] += level.astype(jnp.float32) * scale_s[i, k]
             add(i, k + 1)
 
     def one(i, c):
@@ -211,27 +248,26 @@
     planes, rows, cols = image.shape
     block_rows = width // cols
     per_owner = rows // block_rows
-    per_plane = per_owner * reps
-    within = tile_block % per_plane
-    key = tile_slab[:, 0] * reps + within // per_owner
-    local_id = (tile_block // per_plane) * per_owner + within % per_owner
-    value = local_id * tiles + jnp.arange(tiles, dtype=jnp.int32) + 1
-    meta = jnp.full((8, LANES), -1, jnp.int32).at[0, :tiles].set(key).at[1, :tiles].set(value)
     image2 = image.reshape(planes * rows, cols)
     sens2 = sensitivity.reshape(planes * rows, cols)
     sub = width // LANES
 
     vmem = pl.BlockSpec(memory_space=pltpu.VMEM)
-    hbm = pl.BlockSpec(memory_space=pl.ANY)
-    asked, back = pl.pallas_call(
-        functools.partial(exchange_kernel, (n, reps, tiles, block_rows)),
+    hbm = pl.BlockSpec(memory_space=pltpu.HBM)
+    asked, scale, back = pl.pallas_call(
+        functools.partial(exchange_kernel, (n, reps, tiles, block_rows, per_owner)),
         out_shape=(
             jax.ShapeDtypeStruct((n, LANES), jnp.int32),
-            jax.ShapeDtypeStruct((n * CAP, sub, LANES), jnp.float32),
+            jax.ShapeDtypeStruct((n, LANES), jnp.float32),
+            jax.ShapeDtypeStruct((n * CAP, sub, LANES), jnp.int16),
         ),
-        in_specs=[vmem, hbm, hbm, vmem],
-        out_specs=(vmem, vmem),
+        in_specs=[hbm] * 5,
+        out_specs=(vmem, vmem, vmem),
         scratch_shapes=[
+            pltpu.VMEM((1, tiles), jnp.int32),
+            pltpu.VMEM((1, tiles), jnp.int32),
+            pltpu.VMEM(background.shape, jnp.bfloat16),
+            pltpu.VMEM((n, LANES), jnp.float32),
             pltpu.VMEM(image2.shape, jnp.float32),
             pltpu.VMEM((planes * per_owner, sub, LANES), jnp.bfloat16),
             pltpu.VMEM(system_blocks.shape, jnp.bfloat16),
@@ -242,25 +278,26 @@
             pltpu.SMEM((n, LANES), jnp.int32),
             pltpu.VMEM((n * CAP, sub, LANES), jnp.bfloat16),
             pltpu.VMEM((n * CAP, sub, LANES), jnp.bfloat16),
-            pltpu.VMEM((tiles, sub, LANES), jnp.float32),
-            pltpu.VMEM((n * CAP, sub, LANES), jnp.float32),
-            pltpu.SemaphoreType.DMA((4,)),
+            pltpu.VMEM((tiles, sub, LANES), jnp.int16),
+            pltpu.VMEM((n * CAP, sub, LANES), jnp.int16),
+            pltpu.SemaphoreType.DMA((7,)),
+            pltpu.SemaphoreType.DMA((2,)),
             pltpu.SemaphoreType.DMA((2,)),
             pltpu.SemaphoreType.DMA((2,)),
             pltpu.SemaphoreType.DMA((2,)),
         ],
         compiler_params=pltpu.CompilerParams(
-            collective_id=0, has_side_effects=True, vmem_limit_bytes=48 * 1024 * 1024
+            collective_id=0, has_side_effects=True, vmem_limit_bytes=62914560
         ),
-    )(meta, image2, system_blocks, background)
+    )(tile_slab.reshape(1, tiles), tile_block.reshape(1, tiles), image2, system_blocks, background)
     updated = pl.pallas_call(
         functools.partial(update_kernel, (n, tiles, block_rows)),
         out_shape=jax.ShapeDtypeStruct(image2.shape, jnp.float32),
-        in_specs=[pl.BlockSpec(memory_space=pltpu.SMEM), vmem, vmem, vmem],
+        in_specs=[pl.BlockSpec(memory_space=pltpu.SMEM)] * 2 + [vmem, vmem, vmem],
         out_specs=vmem,
         scratch_shapes=[pltpu.VMEM((planes * per_owner, sub, LANES), jnp.float32)],
         compiler_params=pltpu.CompilerParams(vmem_limit_bytes=48 * 1024 * 1024),
-    )(asked, back, image2, sens2)
+    )(asked, scale, back, image2, sens2)
     return updated.reshape(image.shape)
 
 

time: 51.7 us -> 43 us (0.83)
  Pallas kernels: 45.7 us -> 40.2 us
  local copies, waits for them, and re-layouts: 4.34 us -> 2.43 us
  other arithmetic: 1.34 us -> 0 us
    pallas_call x1, Pallas kernels: 42.7 us -> 36.8 us  [local(): pl.pallas_call(functools.partial(exchange_kernel, (n, reps, tiles, block_...]
    unnamed x10, local copies, waits for them, and re-layouts: 4.15 us -> 2.43 us
    another operation x2 -> x0, other arithmetic: 1.34 us -> none
where the time goes in v2:
time: 43 us; the launch traced here: 42.6 us
  Pallas kernels  40.2 us (93%)
  local copies, waits for them, and re-layouts  2.43 us (6%)
    pallas_call x1, Pallas kernels, local(): pl.pallas_call(functools.partial(exchange_kernel, (n, reps, tiles, block_...  36.8 us
    pallas_call x1, Pallas kernels, local(): pl.pallas_call(functools.partial(update_kernel, (n, tiles, block_rows)),...  3.41 us
    unnamed x10, local copies, waits for them, and re-layouts  2.43 us

profile of v2, /device:TPU:0, one launch (start us, length us, event | category | flops | bytes accessed | tf_op | source)
XLA Modules:
  0.0 42.6 jit_solution(16842040168470781911)
XLA Ops:
  0.0 0.0 copy-start
  0.0 0.0 copy-start.1
  0.0 36.8 %shard_map.64 = (s32[32,128]{1,0:T(8,128)}, f32[32,128]{1,0:T(8,128)}, s16[192,8,128]{2,1,0:T(8,128)(2,1)}) custom-call(s32[1,16]{1,0:T(1,128)} %bitcast.8, s32[1,16]{1,0:T(1,128)} %bitcast.9, f32[1152,256]{1,0:T(8,128)} %bitcast.5, bf16[16,128,1024]{2,1,0:T(8,128)(2,1)} %sys_hbm.1, bf16[16,128]{1,0:T(8,128)(2,1)} %bg_hbm.1), custom_call_target="tpu_custom_call" | custom-call | tf_op jit(solution)/shard_map/pallas_call | solution.py:257
  36.8 0.0 copy-done
  36.8 0.0 copy-done.1
  36.8 0.0 copy-start.2
  36.8 1.0 %copy-done.2 = s16[192,8,128]{2,1,0:T(8,128)(2,1)S(1)} copy-done((s16[192,8,128]{2,1,0:T(8,128)(2,1)S(1)}, s16[192,8,128]{2,1,0:T(8,128)(2,1)}, u32[]{:S(2)}) %copy-start.2) | copy-done | bytes 393240
  37.8 0.0 copy-start.3
  37.8 0.7 %copy-done.3 = s32[32,128]{1,0:T(8,128)S(1)} copy-done((s32[32,128]{1,0:T(8,128)S(1)}, s32[32,128]{1,0:T(8,128)}, u32[]{:S(2)}) %copy-start.3) | copy-done | bytes 16408
  38.5 0.0 copy-start.4
  38.5 0.7 %copy-done.4 = f32[32,128]{1,0:T(8,128)S(1)} copy-done((f32[32,128]{1,0:T(8,128)S(1)}, f32[32,128]{1,0:T(8,128)}, u32[]{:S(2)}) %copy-start.4) | copy-done | bytes 16408
  39.2 3.4 %shard_map.65 = f32[1152,256]{1,0:T(8,128)} custom-call(s32[32,128]{1,0:T(8,128)S(1)} %copy-done.3, f32[32,128]{1,0:T(8,128)S(1)} %copy-done.4, s16[192,8,128]{2,1,0:T(8,128)(2,1)S(1)} %copy-done.2, f32[1152,256]{1,0:T(8,128)S(1)} %bitcast.6, f32[1152,256]{1,0:T(8,128)S(1)} %bitcast.7), custom_call_target="tpu_custom_call" | custom-call | tf_op jit(solution)/shard_map/pallas_call | solution.py:293
Async XLA Ops:
  0.0 36.8 %copy-start = (f32[36,32,256]{2,1,0:T(8,128)S(1)}, f32[36,32,256]{2,1,0:T(8,128)}, u32[]{:S(2)}) copy-start(f32[36,32,256]{2,1,0:T(8,128)} %param.6) | copy-start | bytes 3538948
  0.0 36.8 %copy-start.1 = (f32[36,32,256]{2,1,0:T(8,128)S(1)}, f32[36,32,256]{2,1,0:T(8,128)}, u32[]{:S(2)}) copy-start(f32[36,32,256]{2,1,0:T(8,128)} %param.7) | copy-start | bytes 3538948
  36.8 1.0 %copy-start.2 = (s16[192,8,128]{2,1,0:T(8,128)(2,1)S(1)}, s16[192,8,128]{2,1,0:T(8,128)(2,1)}, u32[]{:S(2)}) copy-start(s16[192,8,128]{2,1,0:T(8,128)(2,1)} %get-tuple-element.10.back_ref) | copy-start | bytes 1179652
  37.8 0.7 %copy-start.3 = (s32[32,128]{1,0:T(8,128)S(1)}, s32[32,128]{1,0:T(8,128)}, u32[]{:S(2)}) copy-start(s32[32,128]{1,0:T(8,128)} %get-tuple-element.8.asked_s) | copy-start | bytes 49156
  38.5 0.7 %copy-start.4 = (f32[32,128]{1,0:T(8,128)S(1)}, f32[32,128]{1,0:T(8,128)}, u32[]{:S(2)}) copy-start(f32[32,128]{1,0:T(8,128)} %get-tuple-element.9.scale_s) | copy-start | bytes 49156

commit v3 on v2

--- a/solution.py
+++ b/solution.py
@@ -22,7 +22,7 @@
 
 def exchange_kernel(
     sizes, slab_hbm, block_hbm, image_hbm, sys_hbm, bg_hbm, asked_ref, scale_ref, back_ref,
-    slab_v, block_v, bg_v, scale_v, image_v, blocks_v, sys_v, mine_v, slot_v, mine_s, slot_s, asked_s, send_f, recv_f, bp_v, send_b,
+    slab_v, block_v, bg_v, scale_v, image_v, blocks_v, sys_v, mine_v, slot_v, mine_s, slot_s, asked_s, send_f, recv_f, sums_v, bp_v, send_b,
     local_sem, id_sem, fetch_sem, back_sem, scale_sem,
 ):
     n, reps, tiles, block_rows, per_owner = sizes
@@ -146,27 +146,30 @@
     others = recv_f.at[pl.ds(CAP, (n - 1) * CAP)]
     pltpu.make_async_copy(others, others, fetch_sem.at[1]).wait()
 
-    peaks = jnp.zeros((1, tiles), jnp.float32)
+    forward = jnp.zeros(background.shape, jnp.float32)
     tile_lane = lax.broadcasted_iota(jnp.int32, (1, tiles), 1)
+    pieces = block_rows * lane_tiles
+    places = [(p % block_rows) * lane_tiles + p // block_rows for p in range(pieces)]
     for t in range(tiles):
         cells = recv_f[slot_s[0, t]].astype(jnp.float32)
         total = None
-        for p in range(block_rows * lane_tiles):
-            q = (p % block_rows) * lane_tiles + p // block_rows
+        for p, q in enumerate(places):
             term = sys_v[t, :, q * LANES:(q + 1) * LANES].astype(jnp.float32) * cells[p:p + 1, :]
             total = term if total is None else total + term
-        forward = jnp.sum(total, axis=1, keepdims=True)
-        inverse = (1.0 / (forward + background[:, t:t + 1])).astype(jnp.bfloat16).astype(jnp.float32)
-        parts = []
-        for p in range(block_rows * lane_tiles):
-            q = (p % block_rows) * lane_tiles + p // block_rows
-            term = sys_v[t, :, q * LANES:(q + 1) * LANES].astype(jnp.float32) * inverse
-            parts.append(jnp.sum(term, axis=0, keepdims=True))
-        tile = jnp.concatenate(parts, axis=0)
-        peak = jnp.maximum(jnp.max(jnp.max(tile, axis=0, keepdims=True), axis=1, keepdims=True), 1e-33)
-        level = jnp.round(tile * (LEVELS / peak)).astype(jnp.int32) - HALF
+        forward = jnp.where(tile_lane == t, jnp.sum(total, axis=1, keepdims=True), forward)
+    inverse = jnp.transpose(1.0 / (forward + background)).astype(jnp.bfloat16)
+    tops = []
+    for t in range(tiles):
+        back = jnp.dot(inverse, sys_v[t], preferred_element_type=jnp.float32)
+        tile = jnp.concatenate([back[t:t + 1, q * LANES:(q + 1) * LANES] for q in places], axis=0)
+        sums_v[t] = tile
+        tops.append(jnp.max(tile, axis=0, keepdims=True))
+    peak = jnp.maximum(jnp.max(jnp.concatenate(tops, axis=0), axis=1, keepdims=True), 1e-33)
+    gain = LEVELS / peak
+    peaks = jnp.transpose(peak)
+    for t in range(tiles):
+        level = jnp.round(sums_v[t] * gain[t:t + 1, :]).astype(jnp.int32) - HALF
         bp_v[t] = jnp.clip(level, -HALF, HALF - 1).astype(jnp.int16)
-        peaks = jnp.where(tile_lane == t, peak, peaks)
     scale_v[...] = tabled(peaks * (1.0 / LEVELS), jnp.float32(0))
 
     def routed(d, k):
@@ -206,8 +209,15 @@
     pltpu.make_async_copy(landed, landed, back_sem.at[1]).wait()
 
 
-def update_kernel(sizes, asked_s, scale_s, back_ref, image_ref, sens_ref, out_ref, sums_v):
+def update_kernel(
+    sizes, asked_hbm, scale_hbm, back_hbm, image_hbm, sens_hbm, out_hbm,
+    asked_s, scale_s, back_ref, image_ref, sens_ref, out_ref, sums_v, in_sem, out_sem,
+):
     n, tiles, block_rows = sizes
+    moves = ((asked_hbm, asked_s), (scale_hbm, scale_s), (back_hbm, back_ref), (image_hbm, image_ref), (sens_hbm, sens_ref))
+    loads = [pltpu.make_async_copy(src, dst, in_sem.at[j]) for j, (src, dst) in enumerate(moves)]
+    for load in loads:
+        load.start()
     lane_tiles = out_ref.shape[1] // LANES
     per_group = 8 // block_rows
     sums_v[...] = jnp.zeros_like(sums_v)
@@ -227,7 +237,11 @@
         add(i, 0)
         return c
 
+    for load in loads[:3]:
+        load.wait()
     lax.fori_loop(0, n, one, 0)
+    for load in loads[3:]:
+        load.wait()
 
     def finish(g, c):
         rows = pl.ds(pl.multiple_of(g * 8, 8), 8)
@@ -238,7 +252,17 @@
             out_ref[rows, cols] = image_ref[rows, cols] * total / sens_ref[rows, cols]
         return c
 
-    lax.fori_loop(0, out_ref.shape[0] // 8, finish, 0, unroll=4)
+    groups = out_ref.shape[0] // 8
+    chunks = out_sem.shape[0]
+    stores = []
+    for c in range(chunks):
+        first, last = groups * c // chunks, groups * (c + 1) // chunks
+        lax.fori_loop(first, last, finish, 0, unroll=4)
+        span = pl.ds(first * 8, (last - first) * 8)
+        stores.append(pltpu.make_async_copy(out_ref.at[span], out_hbm.at[span], out_sem.at[c]))
+        stores[-1].start()
+    for store in stores:
+        store.wait()
 
 
 def local(image, sensitivity, system_blocks, tile_slab, tile_block, background):
@@ -278,6 +302,7 @@
             pltpu.SMEM((n, LANES), jnp.int32),
             pltpu.VMEM((n * CAP, sub, LANES), jnp.bfloat16),
             pltpu.VMEM((n * CAP, sub, LANES), jnp.bfloat16),
+            pltpu.VMEM((tiles, sub, LANES), jnp.float32),
             pltpu.VMEM((tiles, sub, LANES), jnp.int16),
             pltpu.VMEM((n * CAP, sub, LANES), jnp.int16),
             pltpu.SemaphoreType.DMA((7,)),
@@ -287,16 +312,26 @@
             pltpu.SemaphoreType.DMA((2,)),
         ],
         compiler_params=pltpu.CompilerParams(
-            collective_id=0, has_side_effects=True, vmem_limit_bytes=62914560
+            collective_id=0, has_side_effects=True, vmem_limit_bytes=67043328
         ),
     )(tile_slab.reshape(1, tiles), tile_block.reshape(1, tiles), image2, system_blocks, background)
     updated = pl.pallas_call(
         functools.partial(update_kernel, (n, tiles, block_rows)),
         out_shape=jax.ShapeDtypeStruct(image2.shape, jnp.float32),
-        in_specs=[pl.BlockSpec(memory_space=pltpu.SMEM)] * 2 + [vmem, vmem, vmem],
-        out_specs=vmem,
-        scratch_shapes=[pltpu.VMEM((planes * per_owner, sub, LANES), jnp.float32)],
-        compiler_params=pltpu.CompilerParams(vmem_limit_bytes=48 * 1024 * 1024),
+        in_specs=[hbm] * 5,
+        out_specs=hbm,
+        scratch_shapes=[
+            pltpu.SMEM(asked.shape, jnp.int32),
+            pltpu.SMEM(scale.shape, jnp.float32),
+            pltpu.VMEM(back.shape, back.dtype),
+            pltpu.VMEM(image2.shape, jnp.float32),
+            pltpu.VMEM(image2.shape, jnp.float32),
+            pltpu.VMEM(image2.shape, jnp.float32),
+            pltpu.VMEM((planes * per_owner, sub, LANES), jnp.float32),
+            pltpu.SemaphoreType.DMA((5,)),
+            pltpu.SemaphoreType.DMA((4,)),
+        ],
+        compiler_params=pltpu.CompilerParams(vmem_limit_bytes=67043328),
     )(asked, scale, back, image2, sens2)
     return updated.reshape(image.shape)
 

time: 43 us -> 38.7 us (0.900)
  local copies, waits for them, and re-layouts: 2.43 us -> 0 us
  Pallas kernels: 40.2 us -> 38.5 us
    unnamed x10 -> x0, local copies, waits for them, and re-layouts: 2.43 us -> none
    pallas_call x1, Pallas kernels: 36.8 us -> 35.3 us  [local(): pl.pallas_call(functools.partial(exchange_kernel, (n, reps, tiles, block_...]
where the time goes in v3:
time: 38.7 us; the launch traced here: 38.5 us
  Pallas kernels  38.5 us (99%)
    pallas_call x1, Pallas kernels, local(): pl.pallas_call(functools.partial(exchange_kernel, (n, reps, tiles, block_...  35.3 us
    pallas_call x1, Pallas kernels, local(): pl.pallas_call(functools.partial(update_kernel, (n, tiles, block_rows)),...  3.14 us

profile of v3, /device:TPU:0, one launch (start us, length us, event | category | flops | bytes accessed | tf_op | source)
XLA Modules:
  0.0 38.5 jit_solution(11759471224969786430)
XLA Ops:
  0.0 35.3 %shard_map.64 = (s32[32,128]{1,0:T(8,128)}, f32[32,128]{1,0:T(8,128)}, s16[192,8,128]{2,1,0:T(8,128)(2,1)}) custom-call(s32[1,16]{1,0:T(1,128)} %bitcast.8, s32[1,16]{1,0:T(1,128)} %bitcast.9, f32[1152,256]{1,0:T(8,128)} %bitcast.5, bf16[16,128,1024]{2,1,0:T(8,128)(2,1)} %sys_hbm.1, bf16[16,128]{1,0:T(8,128)(2,1)} %bg_hbm.1), custom_call_target="tpu_custom_call" | custom-call | tf_op jit(solution)/shard_map/pallas_call | solution.py:281
  35.3 3.1 %shard_map.65 = f32[1152,256]{1,0:T(8,128)} custom-call(s32[32,128]{1,0:T(8,128)} %get-tuple-element.8.asked_hbm, f32[32,128]{1,0:T(8,128)} %get-tuple-element.9.scale_hbm, s16[192,8,128]{2,1,0:T(8,128)(2,1)} %get-tuple-element.10.back_hbm, f32[1152,256]{1,0:T(8,128)} %bitcast.6, f32[1152,256]{1,0:T(8,128)} %bitcast.7), custom_call_target="tpu_custom_call" | custom-call | tf_op jit(solution)/shard_map/pallas_call | solution.py:318

commit v4 on v3

--- a/solution.py
+++ b/solution.py
@@ -30,7 +30,7 @@
     lane_tiles = image_v.shape[1] // LANES
 
     def device(d):
-        return (d // reps, d % reps)
+        return (lax.div(d, reps), lax.rem(d, reps))
 
     load_sys = pltpu.make_async_copy(sys_hbm, sys_v, local_sem.at[0])
     load_image = pltpu.make_async_copy(image_hbm, image_v, local_sem.at[1])
@@ -43,7 +43,7 @@
     barrier = pltpu.get_barrier_semaphore()
 
     def greet(i, c):
-        pl.semaphore_signal(barrier, inc=1, device_id=device((me + i) % n), device_id_type=MESH)
+        pl.semaphore_signal(barrier, inc=1, device_id=device(lax.rem(me + i, n)), device_id_type=MESH)
         return c
 
     lax.fori_loop(1, n, greet, 0)
@@ -86,7 +86,7 @@
     pl.semaphore_wait(barrier, n - 1)
 
     def id_copy(i):
-        d = (me + i) % n
+        d = lax.rem(me + i, n)
         return pltpu.make_async_remote_copy(
             src_ref=mine_v.at[pl.ds(d, 1)], dst_ref=asked_ref.at[pl.ds(i, 1)],
             send_sem=id_sem.at[0], recv_sem=id_sem.at[1],
@@ -123,7 +123,7 @@
     to_asked.wait()
 
     def served(i, k):
-        return blocks_v[jnp.maximum(asked_s[i, k] - 1, 0) // tiles]
+        return blocks_v[split(jnp.maximum(asked_s[i, k] - 1, 0), tiles)[0]]
 
     for k in range(CAP):
         recv_f[k] = served(0, k)
@@ -135,7 +135,7 @@
         pltpu.make_async_remote_copy(
             src_ref=send_f.at[span], dst_ref=recv_f.at[span],
             send_sem=fetch_sem.at[0], recv_sem=fetch_sem.at[1],
-            device_id=device((me + n - i) % n), device_id_type=MESH,
+            device_id=device(lax.rem(me + n - i, n)), device_id_type=MESH,
         ).start()
         return c
 
@@ -173,13 +173,13 @@
     scale_v[...] = tabled(peaks * (1.0 / LEVELS), jnp.float32(0))
 
     def routed(d, k):
-        return bp_v[jnp.maximum(mine_s[d, k] - 1, 0) % tiles]
+        return bp_v[split(jnp.maximum(mine_s[d, k] - 1, 0), tiles)[1]]
 
     for k in range(CAP):
         back_ref[k] = routed(me, k)
 
     def give(i, c):
-        d = (me + i) % n
+        d = lax.rem(me + i, n)
         for k in range(CAP):
             send_b[i * CAP + k] = routed(d, k)
         span = pl.ds(i * CAP, CAP)
@@ -230,7 +230,7 @@
         @pl.when(value > 0)
         def _():
             level = back_ref[i * CAP + k].astype(jnp.int32) + HALF
-            sums_v[(value - 1) // tiles] += level.astype(jnp.float32) * scale_s[i, k]
+            sums_v[split(value - 1, tiles)[0]] += level.astype(jnp.float32) * scale_s[i, k]
             add(i, k + 1)
 
     def one(i, c):

time: 38.7 us -> 38.4 us (level)
  Pallas kernels: 38.5 us -> 38.1 us
where the time goes in v4:
time: 38.4 us; the launch traced here: 38.2 us
  Pallas kernels  38.1 us (99%)
    pallas_call x1, Pallas kernels, local(): pl.pallas_call(functools.partial(exchange_kernel, (n, reps, tiles, block_...  35 us
    pallas_call x1, Pallas kernels, local(): pl.pallas_call(functools.partial(update_kernel, (n, tiles, block_rows)),...  3.18 us

profile of v4, /device:TPU:0, one launch (start us, length us, event | category | flops | bytes accessed | tf_op | source)
XLA Modules:
  0.0 38.2 jit_solution(2653960126441831474)
XLA Ops:
  0.0 35.0 %shard_map.64 = (s32[32,128]{1,0:T(8,128)}, f32[32,128]{1,0:T(8,128)}, s16[192,8,128]{2,1,0:T(8,128)(2,1)}) custom-call(s32[1,16]{1,0:T(1,128)} %bitcast.8, s32[1,16]{1,0:T(1,128)} %bitcast.9, f32[1152,256]{1,0:T(8,128)} %bitcast.5, bf16[16,128,1024]{2,1,0:T(8,128)(2,1)} %sys_hbm.1, bf16[16,128]{1,0:T(8,128)(2,1)} %bg_hbm.1), custom_call_target="tpu_custom_call" | custom-call | tf_op jit(solution)/shard_map/pallas_call | solution.py:281
  35.0 3.2 %shard_map.65 = f32[1152,256]{1,0:T(8,128)} custom-call(s32[32,128]{1,0:T(8,128)} %get-tuple-element.8.asked_hbm, f32[32,128]{1,0:T(8,128)} %get-tuple-element.9.scale_hbm, s16[192,8,128]{2,1,0:T(8,128)(2,1)} %get-tuple-element.10.back_hbm, f32[1152,256]{1,0:T(8,128)} %bitcast.6, f32[1152,256]{1,0:T(8,128)} %bitcast.7), custom_call_target="tpu_custom_call" | custom-call | tf_op jit(solution)/shard_map/pallas_call | solution.py:318

commit v5 on v4

--- a/solution.py
+++ b/solution.py
@@ -21,8 +21,8 @@
 
 
 def exchange_kernel(
-    sizes, slab_hbm, block_hbm, image_hbm, sys_hbm, bg_hbm, asked_ref, scale_ref, back_ref,
-    slab_v, block_v, bg_v, scale_v, image_v, blocks_v, sys_v, mine_v, slot_v, mine_s, slot_s, asked_s, send_f, recv_f, sums_v, bp_v, send_b,
+    sizes, slab_hbm, block_hbm, image_hbm, sys_hbm, bg_hbm, asked_hbm, scale_ref, back_ref,
+    asked_ref, slab_v, block_v, bg_v, scale_v, image_v, blocks_v, sys_v, mine_v, slot_v, mine_s, slot_s, asked_s, send_f, recv_f, sums_v, bp_v, send_b,
     local_sem, id_sem, fetch_sem, back_sem, scale_sem,
 ):
     n, reps, tiles, block_rows, per_owner = sizes
@@ -120,6 +120,8 @@
     pltpu.make_async_copy(rest, rest, id_sem.at[1]).wait()
     to_asked = pltpu.make_async_copy(asked_ref, asked_s, local_sem.at[2])
     to_asked.start()
+    keep_asked = pltpu.make_async_copy(asked_ref, asked_hbm, local_sem.at[3])
+    keep_asked.start()
     to_asked.wait()
 
     def served(i, k):
@@ -176,7 +178,11 @@
         return bp_v[split(jnp.maximum(mine_s[d, k] - 1, 0), tiles)[1]]
 
     for k in range(CAP):
-        back_ref[k] = routed(me, k)
+        send_b[k] = routed(me, k)
+    own_back = pltpu.make_async_copy(send_b.at[pl.ds(0, CAP)], back_ref.at[pl.ds(0, CAP)], local_sem.at[4])
+    own_back.start()
+    own_scale = pltpu.make_async_copy(scale_v.at[pl.ds(me, 1)], scale_ref.at[pl.ds(0, 1)], local_sem.at[5])
+    own_scale.start()
 
     def give(i, c):
         d = lax.rem(me + i, n)
@@ -195,8 +201,9 @@
         ).start()
         return c
 
-    scale_ref[pl.ds(0, 1), :] = scale_v[pl.ds(me, 1), :]
     lax.fori_loop(1, n, give, 0)
+    for copy in (keep_asked, own_back, own_scale):
+        copy.wait()
     scaled = scale_ref.at[pl.ds(1, n - 1)]
     pltpu.make_async_copy(scaled, scaled, scale_sem.at[0]).wait()
     pltpu.make_async_copy(scaled, scaled, scale_sem.at[1]).wait()
@@ -276,7 +283,6 @@
     sens2 = sensitivity.reshape(planes * rows, cols)
     sub = width // LANES
 
-    vmem = pl.BlockSpec(memory_space=pltpu.VMEM)
     hbm = pl.BlockSpec(memory_space=pltpu.HBM)
     asked, scale, back = pl.pallas_call(
         functools.partial(exchange_kernel, (n, reps, tiles, block_rows, per_owner)),
@@ -286,8 +292,9 @@
             jax.ShapeDtypeStruct((n * CAP, sub, LANES), jnp.int16),
         ),
         in_specs=[hbm] * 5,
-        out_specs=(vmem, vmem, vmem),
+        out_specs=(hbm, hbm, hbm),
         scratch_shapes=[
+            pltpu.VMEM((n, LANES), jnp.int32),
             pltpu.VMEM((1, tiles), jnp.int32),
             pltpu.VMEM((1, tiles), jnp.int32),
             pltpu.VMEM(background.shape, jnp.bfloat16),

time: 38.4 us -> 37.7 us (0.982)
  Pallas kernels: 38.1 us -> 37.4 us
    pallas_call x1, Pallas kernels: 35 us -> 34.3 us  [local(): pl.pallas_call(functools.partial(exchange_kernel, (n, reps, tiles, block_...]
where the time goes in v5:
time: 37.7 us; the launch traced here: 37.4 us
  Pallas kernels  37.4 us (99%)
    pallas_call x1, Pallas kernels, local(): pl.pallas_call(functools.partial(exchange_kernel, (n, reps, tiles, block_...  34.3 us
    pallas_call x1, Pallas kernels, local(): pl.pallas_call(functools.partial(update_kernel, (n, tiles, block_rows)),...  3.09 us

profile of v5, /device:TPU:0, one launch (start us, length us, event | category | flops | bytes accessed | tf_op | source)
XLA Modules:
  0.0 37.4 jit_solution(13951011418600396769)
XLA Ops:
  0.0 34.3 %shard_map.64 = (s32[32,128]{1,0:T(8,128)}, f32[32,128]{1,0:T(8,128)}, s16[192,8,128]{2,1,0:T(8,128)(2,1)}) custom-call(s32[1,16]{1,0:T(1,128)} %bitcast.8, s32[1,16]{1,0:T(1,128)} %bitcast.9, f32[1152,256]{1,0:T(8,128)} %bitcast.5, bf16[16,128,1024]{2,1,0:T(8,128)(2,1)} %sys_hbm.1, bf16[16,128]{1,0:T(8,128)(2,1)} %bg_hbm.1), custom_call_target="tpu_custom_call" | custom-call | tf_op jit(solution)/shard_map/pallas_call | solution.py:287
  34.3 3.1 %shard_map.65 = f32[1152,256]{1,0:T(8,128)} custom-call(s32[32,128]{1,0:T(8,128)} %get-tuple-element.8.asked_hbm, f32[32,128]{1,0:T(8,128)} %get-tuple-element.9.scale_hbm, s16[192,8,128]{2,1,0:T(8,128)(2,1)} %get-tuple-element.10.back_hbm, f32[1152,256]{1,0:T(8,128)} %bitcast.6, f32[1152,256]{1,0:T(8,128)} %bitcast.7), custom_call_target="tpu_custom_call" | custom-call | tf_op jit(solution)/shard_map/pallas_call | solution.py:325

commit v6 on v5

--- a/solution.py
+++ b/solution.py
@@ -130,7 +130,14 @@
     for k in range(CAP):
         recv_f[k] = served(0, k)
 
-    def serve(i, c):
+    def far_first(j):
+        return lax.rem(j, slabs) * reps + lax.rem(reps // 2 + lax.div(j, slabs), reps)
+
+    slabs = n // reps
+    own_turn = (reps - reps // 2) * slabs
+
+    def serve(j, c):
+        i = far_first(j)
         for k in range(CAP):
             send_f[i * CAP + k] = served(i, k)
         span = pl.ds(i * CAP, CAP)
@@ -141,7 +148,8 @@
         ).start()
         return c
 
-    lax.fori_loop(1, n, serve, 0)
+    lax.fori_loop(0, own_turn, serve, 0)
+    lax.fori_loop(own_turn + 1, n, serve, 0)
     load_bg.wait()
     background = jnp.transpose(bg_v[...].astype(jnp.float32))
     load_sys.wait()
@@ -184,7 +192,8 @@
     own_scale = pltpu.make_async_copy(scale_v.at[pl.ds(me, 1)], scale_ref.at[pl.ds(0, 1)], local_sem.at[5])
     own_scale.start()
 
-    def give(i, c):
+    def give(j, c):
+        i = far_first(j)
         d = lax.rem(me + i, n)
         for k in range(CAP):
             send_b[i * CAP + k] = routed(d, k)
@@ -201,7 +210,8 @@
         ).start()
         return c
 
-    lax.fori_loop(1, n, give, 0)
+    lax.fori_loop(0, own_turn, give, 0)
+    lax.fori_loop(own_turn + 1, n, give, 0)
     for copy in (keep_asked, own_back, own_scale):
         copy.wait()
     scaled = scale_ref.at[pl.ds(1, n - 1)]

time: 37.7 us -> 37.5 us (level)
  no operation moved by 1% of the time
where the time goes in v6:
time: 37.5 us; the launch traced here: 37.2 us
  Pallas kernels  37.2 us (99%)
    pallas_call x1, Pallas kernels, local(): pl.pallas_call(functools.partial(exchange_kernel, (n, reps, tiles, block_...  34.1 us
    pallas_call x1, Pallas kernels, local(): pl.pallas_call(functools.partial(update_kernel, (n, tiles, block_rows)),...  3.15 us

profile of v6, /device:TPU:0, one launch (start us, length us, event | category | flops | bytes accessed | tf_op | source)
XLA Modules:
  0.0 37.2 jit_solution(6938483590880140734)
XLA Ops:
  0.0 34.1 %shard_map.64 = (s32[32,128]{1,0:T(8,128)}, f32[32,128]{1,0:T(8,128)}, s16[192,8,128]{2,1,0:T(8,128)(2,1)}) custom-call(s32[1,16]{1,0:T(1,128)} %bitcast.8, s32[1,16]{1,0:T(1,128)} %bitcast.9, f32[1152,256]{1,0:T(8,128)} %bitcast.5, bf16[16,128,1024]{2,1,0:T(8,128)(2,1)} %sys_hbm.1, bf16[16,128]{1,0:T(8,128)(2,1)} %bg_hbm.1), custom_call_target="tpu_custom_call" | custom-call | tf_op jit(solution)/shard_map/pallas_call | solution.py:297
  34.1 3.2 %shard_map.65 = f32[1152,256]{1,0:T(8,128)} custom-call(s32[32,128]{1,0:T(8,128)} %get-tuple-element.8.asked_hbm, f32[32,128]{1,0:T(8,128)} %get-tuple-element.9.scale_hbm, s16[192,8,128]{2,1,0:T(8,128)(2,1)} %get-tuple-element.10.back_hbm, f32[1152,256]{1,0:T(8,128)} %bitcast.6, f32[1152,256]{1,0:T(8,128)} %bitcast.7), custom_call_target="tpu_custom_call" | custom-call | tf_op jit(solution)/shard_map/pallas_call | solution.py:335
